TPU v7x, 32 devices: a whole 2x2x4 slice. The times are simulated.
32 devices in a mesh: dev: 32 (over z, y, x, core).
Axes of the slice: x: 2, y: 2, z: 4, core: 2. Of those that a mesh axis runs over, the one named last changes fastest.
Arguments:
- source: bfloat16 [48, 262144], P(None, 'dev'), may hold values from -6 to 6
- weights: bfloat16 [20480, 128, 128], P('dev'), may hold values from -0.01953125 to 0.01953125
- tile_map: int32 [3, 20480], P(None, 'dev'), may hold values from 0 to 63, as said below
- tile_count: int32 [32], P('dev'), may hold values from 160 to 640, as said below
Outputs:
- acoustic_source: float32 [48, 4096], P(None, 'dev')
Inputs may be any that keep to these rules, and one draw needn't show every extreme that they name: `tile_map`: row 0 is a CFD block of the owning device; row 2 an acoustic block of the destination. Row 1 is a device at cyclic distance at most 4 from the owner in device order, or at distance exactly 32 // 2 (counted upward); every device has used slots at distance +4, -4 and 32 // 2. `tile_count`: some device uses all its slots.
All inputs are finite; a program needn't handle non-finite values.
Results may differ from a plain program's by a relative error of at most 0.0003.
Values sent between devices are 32-bit elements; how exact they have to be, the bound alone decides.
A program may use at most 128 MiB of HBM per device.

v0:
```python
import jax
import jax.numpy as jnp
from jax import lax
from jax.sharding import PartitionSpec as P

REACH = 4
ACU_BLK_DEV = 1


def passed_along(value, axis, steps):
    count = lax.axis_size(axis)
    pairs = [(source, (source + steps) % count) for source in range(count)]
    return lax.ppermute(value, axis, pairs)


def on_device(source, weights, tile_map, tile_count):
    feat, cells = source.shape
    tiles, blk_size = (weights.shape[0], weights.shape[1])
    acu = ACU_BLK_DEV
    blocks = source.reshape(feat, cells // blk_size, blk_size)
    picked = jnp.take(blocks, tile_map[0], axis=1)
    products = jnp.einsum("ftc,tcn->tfn", picked, weights, preferred_element_type=jnp.float32)
    used = jnp.arange(tiles, dtype=jnp.int32) < tile_count[0]
    products = jnp.where(used[:, None, None], products, 0.0)
    devices = lax.axis_size("dev")
    own = lax.axis_index("dev")
    half_way = devices // 2
    upward = (tile_map[1] - own) % devices
    distance = jnp.where(upward > half_way, upward - devices, upward)
    far_slot = 2 * REACH + 1
    is_far = jnp.logical_and(upward == half_way, half_way > REACH)
    slot_key = jnp.where(is_far, far_slot, distance + REACH)
    segment_key = slot_key * acu + tile_map[2]
    outgoing = jax.ops.segment_sum(products, segment_key, num_segments=(2 * REACH + 2) * acu)
    outgoing = outgoing.reshape(2 * REACH + 2, acu, feat, blk_size)
    total = outgoing[REACH]
    for index in range(2 * REACH + 1):
        if index != REACH:
            total = total + passed_along(outgoing[index], "dev", index - REACH)
    total = total + passed_along(outgoing[far_slot], "dev", half_way)
    return jnp.transpose(total, (1, 0, 2)).reshape(feat, acu * blk_size)


def solution(mesh):
    return jax.shard_map(
        on_device,
        mesh=mesh,
        in_specs=(P(None, "dev"), P("dev", None, None), P(None, "dev"), P("dev")),
        out_specs=P(None, "dev"),
        check_vma=False,
    )
```

profile of v0, /device:TPU:0, one launch (start us, length us, event | category | flops | bytes accessed | tf_op | source)
XLA Modules:
  0.0 105.4 jit_solution(12443748260390171646)
XLA Ops:
  0.0 0.0 copy-start
  0.0 0.8 slice_reduce_fusion
  0.8 0.9 fusion.13
  1.7 0.0 copy-done
  1.7 0.1 copy_bitcast_fusion
  2.5 4.8 %gather_fusion = bf16[640,48,128]{2,1,0:T(8,128)(2,1)} fusion(bf16[48,64,128]{2,0,1:T(8,128)(2,1)S(1)} %copy_bitcast_fusion, s32[1024]{0:T(1024)S(1)} %pad_clamp_fusion), kind=kCustom, calls=%fused_computation | custom fusion | bytes 15731200 | tf_op jit(solution)/shard_map/jit(_take)/gather | solution.py:21
  7.2 16.4 %convolution_select_fusion = f32[640,48,128]{2,1,0:T(8,128)} fusion(bf16[640,128,128]{2,1,0:T(8,128)(2,1)} %param.5, bf16[640,48,128]{2,1,0:T(8,128)(2,1)} %gather_fusion, pred[640]{0:T(1024)(128)(4,1)S(1)} %get-tuple-element.17, pred[640]{0:T(1024)(128)(4,1)S(1)} %get-tuple-element.16), kind=kOutput, calls=%fused_computation.2 | convolution fusion | flops 1014497280 | bytes 44565760 | tf_op jit(solution)/shard_map/ftc,tcn->tfn/dot_general | solution.py:22
  23.6 62.2 %scatter_fusion = f32[10,48,128]{2,1,0:T(8,128)S(1)} fusion(f32[10,48,128]{2,1,0:T(8,128)S(1)} %broadcast_in_dim.31, s32[640]{0:T(1024)S(1)} %get-tuple-element.6, f32[640,48,128]{2,1,0:T(8,128)} %convolution_select_fusion), kind=kCustom, calls=%fused_computation.1 | custom fusion | flops 3932160 | bytes 47188480 | tf_op jit(solution)/shard_map/scatter-add | solution.py:34
  85.9 6.1 %collective-permute-start = (f32[1,48,128]{2,1,0:T(8,128)S(1)}, f32[1,48,128]{2,1,0:T(8,128)S(1)}, u32[]{:S(2)}, u32[]{:S(2)}) collective-permute-start(f32[1,48,128]{2,1,0:T(8,128)S(1)} %get-tuple-element.7), channel_id=1, source_target_pairs={{0,28},{1,29},{2,30},{3,31},{4,0},{5,1},{6,2},{7,3},{8,4},{9,5},{1... | collective-permute-start | bytes 73736 | tf_op jit(solution)/shard_map/ppermute | solution.py:13
  92.0 0.0 collective-permute-start.1
  92.0 2.0 %collective-permute-start.2 = (f32[1,48,128]{2,1,0:T(8,128)S(1)}, f32[1,48,128]{2,1,0:T(8,128)S(1)}, u32[]{:S(2)}, u32[]{:S(2)}) collective-permute-start(f32[1,48,128]{2,1,0:T(8,128)S(1)} %get-tuple-element.14), channel_id=1, source_target_pairs={{0,30},{1,31},{2,0},{3,1},{4,2},{5,3},{6,4},{7,5},{8,6},{9,7},{10,... | collective-permute-start | bytes 73736 | tf_op jit(solution)/shard_map/ppermute | solution.py:13
  93.9 1.8 %collective-permute-start.3 = (f32[1,48,128]{2,1,0:T(8,128)S(1)}, f32[1,48,128]{2,1,0:T(8,128)S(1)}, u32[]{:S(2)}, u32[]{:S(2)}) collective-permute-start(f32[1,48,128]{2,1,0:T(8,128)S(1)} %get-tuple-element.13), channel_id=1, source_target_pairs={{0,31},{1,0},{2,1},{3,2},{4,3},{5,4},{6,5},{7,6},{8,7},{9,8},{10,9... | collective-permute-start | bytes 73736 | tf_op jit(solution)/shard_map/ppermute | solution.py:13
  95.7 0.0 collective-permute-start.4
  95.7 0.0 collective-permute-done
  95.7 0.0 collective-permute-start.5
  95.7 0.0 collective-permute-done.1
  95.7 2.1 %collective-permute-start.6 = (f32[1,48,128]{2,1,0:T(8,128)S(1)}, f32[1,48,128]{2,1,0:T(8,128)S(1)}, u32[]{:S(2)}, u32[]{:S(2)}) collective-permute-start(f32[1,48,128]{2,1,0:T(8,128)S(1)} %get-tuple-element.10), channel_id=1, source_target_pairs={{0,3},{1,4},{2,5},{3,6},{4,7},{5,8},{6,9},{7,10},{8,11},{9,12},{10... | collective-permute-start | bytes 73736 | tf_op jit(solution)/shard_map/ppermute | solution.py:13
  97.8 0.0 collective-permute-done.2
  97.8 2.2 %collective-permute-start.7 = (f32[1,48,128]{2,1,0:T(8,128)S(1)}, f32[1,48,128]{2,1,0:T(8,128)S(1)}, u32[]{:S(2)}, u32[]{:S(2)}) collective-permute-start(f32[1,48,128]{2,1,0:T(8,128)S(1)} %get-tuple-element.9), channel_id=1, source_target_pairs={{0,4},{1,5},{2,6},{3,7},{4,8},{5,9},{6,10},{7,11},{8,12},{9,13},{1... | collective-permute-start | bytes 73736 | tf_op jit(solution)/shard_map/ppermute | solution.py:13
  100.0 0.0 collective-permute-done.3
  100.0 0.0 collective-permute-start.8
  100.0 2.5 %collective-permute-done.4 = f32[1,48,128]{2,1,0:T(8,128)S(1)} collective-permute-done((f32[1,48,128]{2,1,0:T(8,128)S(1)}, f32[1,48,128]{2,1,0:T(8,128)S(1)}, u32[]{:S(2)}, u32[]{:S(2)}) %collective-permute-start.4) | collective-permute-done | bytes 24608 | tf_op jit(solution)/shard_map/ppermute | solution.py:13
  102.6 1.1 collective-permute-done.5
  103.6 0.0 collective-permute-done.6
  103.6 0.8 collective-permute-done.7
  104.4 0.3 collective-permute-done.8
  104.7 0.6 fusion.12
  (4 shorter events, 0.0 us)
Async XLA Ops:
  0.0 1.7 %copy-start = (bf16[48,8192]{1,0:T(8,128)(2,1)S(1)}, bf16[48,8192]{1,0:T(8,128)(2,1)}, u32[]{:S(2)}) copy-start(bf16[48,8192]{1,0:T(8,128)(2,1)} %param.4) | copy-start | bytes 2359300
  85.9 9.9 %collective-permute-start = (f32[1,48,128]{2,1,0:T(8,128)S(1)}, f32[1,48,128]{2,1,0:T(8,128)S(1)}, u32[]{:S(2)}, u32[]{:S(2)}) collective-permute-start(f32[1,48,128]{2,1,0:T(8,128)S(1)} %get-tuple-element.7), channel_id=1, source_target_pairs={{0,28},{1,29},{2,30},{3,31},{4,0},{5,1},{6,2},{7,3},{8,4},{9,5},{1... | collective-permute-start | bytes 73736 | tf_op jit(solution)/shard_map/ppermute | solution.py:13
  92.0 3.8 %collective-permute-start.1 = (f32[1,48,128]{2,1,0:T(8,128)S(1)}, f32[1,48,128]{2,1,0:T(8,128)S(1)}, u32[]{:S(2)}, u32[]{:S(2)}) collective-permute-start(f32[1,48,128]{2,1,0:T(8,128)S(1)} %get-tuple-element.15), channel_id=1, source_target_pairs={{0,29},{1,30},{2,31},{3,0},{4,1},{5,2},{6,3},{7,4},{8,5},{9,6},{10... | collective-permute-start | bytes 73736 | tf_op jit(solution)/shard_map/ppermute | solution.py:13
  92.0 5.9 %collective-permute-start.2 = (f32[1,48,128]{2,1,0:T(8,128)S(1)}, f32[1,48,128]{2,1,0:T(8,128)S(1)}, u32[]{:S(2)}, u32[]{:S(2)}) collective-permute-start(f32[1,48,128]{2,1,0:T(8,128)S(1)} %get-tuple-element.14), channel_id=1, source_target_pairs={{0,30},{1,31},{2,0},{3,1},{4,2},{5,3},{6,4},{7,5},{8,6},{9,7},{10,... | collective-permute-start | bytes 73736 | tf_op jit(solution)/shard_map/ppermute | solution.py:13
  93.9 6.1 %collective-permute-start.3 = (f32[1,48,128]{2,1,0:T(8,128)S(1)}, f32[1,48,128]{2,1,0:T(8,128)S(1)}, u32[]{:S(2)}, u32[]{:S(2)}) collective-permute-start(f32[1,48,128]{2,1,0:T(8,128)S(1)} %get-tuple-element.13), channel_id=1, source_target_pairs={{0,31},{1,0},{2,1},{3,2},{4,3},{5,4},{6,5},{7,6},{8,7},{9,8},{10,9... | collective-permute-start | bytes 73736 | tf_op jit(solution)/shard_map/ppermute | solution.py:13
  95.7 6.8 %collective-permute-start.4 = (f32[1,48,128]{2,1,0:T(8,128)S(1)}, f32[1,48,128]{2,1,0:T(8,128)S(1)}, u32[]{:S(2)}, u32[]{:S(2)}) collective-permute-start(f32[1,48,128]{2,1,0:T(8,128)S(1)} %get-tuple-element.12), channel_id=1, source_target_pairs={{0,1},{1,2},{2,3},{3,4},{4,5},{5,6},{6,7},{7,8},{8,9},{9,10},{10,1... | collective-permute-start | bytes 73736 | tf_op jit(solution)/shard_map/ppermute | solution.py:13
  95.7 7.9 %collective-permute-start.5 = (f32[1,48,128]{2,1,0:T(8,128)S(1)}, f32[1,48,128]{2,1,0:T(8,128)S(1)}, u32[]{:S(2)}, u32[]{:S(2)}) collective-permute-start(f32[1,48,128]{2,1,0:T(8,128)S(1)} %get-tuple-element.11), channel_id=1, source_target_pairs={{0,2},{1,3},{2,4},{3,5},{4,6},{5,7},{6,8},{7,9},{8,10},{9,11},{10,... | collective-permute-start | bytes 73736 | tf_op jit(solution)/shard_map/ppermute | solution.py:13
  95.7 7.9 %collective-permute-start.6 = (f32[1,48,128]{2,1,0:T(8,128)S(1)}, f32[1,48,128]{2,1,0:T(8,128)S(1)}, u32[]{:S(2)}, u32[]{:S(2)}) collective-permute-start(f32[1,48,128]{2,1,0:T(8,128)S(1)} %get-tuple-element.10), channel_id=1, source_target_pairs={{0,3},{1,4},{2,5},{3,6},{4,7},{5,8},{6,9},{7,10},{8,11},{9,12},{10... | collective-permute-start | bytes 73736 | tf_op jit(solution)/shard_map/ppermute | solution.py:13
  97.8 6.6 %collective-permute-start.7 = (f32[1,48,128]{2,1,0:T(8,128)S(1)}, f32[1,48,128]{2,1,0:T(8,128)S(1)}, u32[]{:S(2)}, u32[]{:S(2)}) collective-permute-start(f32[1,48,128]{2,1,0:T(8,128)S(1)} %get-tuple-element.9), channel_id=1, source_target_pairs={{0,4},{1,5},{2,6},{3,7},{4,8},{5,9},{6,10},{7,11},{8,12},{9,13},{1... | collective-permute-start | bytes 73736 | tf_op jit(solution)/shard_map/ppermute | solution.py:13
  100.0 4.7 %collective-permute-start.8 = (f32[1,48,128]{2,1,0:T(8,128)S(1)}, f32[1,48,128]{2,1,0:T(8,128)S(1)}, u32[]{:S(2)}, u32[]{:S(2)}) collective-permute-start(f32[1,48,128]{2,1,0:T(8,128)S(1)} %get-tuple-element.8), channel_id=1, source_target_pairs={{0,16},{1,17},{2,18},{3,19},{4,20},{5,21},{6,22},{7,23},{8,24},{9,... | collective-permute-start | bytes 73736 | tf_op jit(solution)/shard_map/ppermute | solution.py:13
where the time goes:
time: 107 us; the launch traced here: 105 us
  other arithmetic  63.7 us (60%)
  matrix products  16.4 us (15%)
  starting transfers between devices  14.1 us (13%)
  local copies, waits for them, and re-layouts  5.74 us (5%)
  waiting for transfers between devices  4.73 us (4%)
    scatter-add x1, other arithmetic, on_device(): jax.ops.segment_sum(products, segment_key, num_segments=(2 * REACH + 2) *...  62.2 us
    dot_general x1, matrix products, on_device(): jnp.einsum('ftc,tcn->tfn', picked, weights, preferred_element_type=jnp.fl...  16.4 us
    ppermute x9, starting transfers between devices, passed_along(): return lax.ppermute(value, axis, pairs)  14.1 us
    gather x1, local copies, waits for them, and re-layouts, on_device(): picked = jnp.take(blocks, tile_map[0], axis=1)  4.78 us
    ppermute x9, waiting for transfers between devices, passed_along(): return lax.ppermute(value, axis, pairs)  4.73 us
  transfers between devices with their start and end apart: 9, of which 4 were waited for; matrix products, arithmetic and copies ran while one was open for 0% of the time, Pallas kernels for 0%

commit v1 on v0

v1 whole, which is shorter than its diff:
```python
import functools

import jax
import jax.numpy as jnp
from jax import lax
from jax.experimental import pallas as pl
from jax.experimental.pallas import tpu as pltpu
from jax.sharding import PartitionSpec as P

REACH = 4
ACU_BLK_DEV = 1
CHUNK = 32
COPIES = 8


def passed_along(value, axis, steps):
    count = lax.axis_size(axis)
    pairs = [(source, (source + steps) % count) for source in range(count)]
    return lax.ppermute(value, axis, pairs)


def sums_kernel(devices, chunk, map_ref, count_ref, src_hbm, w_hbm, out_ref, src, w, lut, src_sem, w_sem, *accs):
    tiles, blk, _ = w_hbm.shape
    slots = out_ref.shape[0]
    own = lax.axis_index("dev")
    count = count_ref[0]
    trips = lax.div(count + (chunk - 1), chunk)

    def chunk_copy(c):
        rows = pl.ds(pl.multiple_of(c * chunk, chunk), chunk)
        return pltpu.make_async_copy(w_hbm.at[rows], w.at[rows], w_sem.at[c])

    src_copy = pltpu.make_async_copy(src_hbm, src, src_sem)
    src_copy.start()

    @pl.loop(0, trips)
    def _(c):
        chunk_copy(c).start()

    for slot in range(2 * REACH + 1):
        lut[lax.rem(own + (slot - REACH) + devices, devices)] = slot
    if devices // 2 > REACH:
        lut[lax.rem(own + devices // 2, devices)] = 2 * REACH + 1

    for acc in accs:
        acc[...] = jnp.zeros_like(acc)
    src_copy.wait()

    @pl.loop(0, trips)
    def _(c):
        chunk_copy(c).wait()
        for j in range(chunk):
            t = c * chunk + j
            begin = pl.multiple_of(map_ref[0, t] * blk, blk)
            key = lut[map_ref[1, t]]
            if ACU_BLK_DEV > 1:
                key = key * ACU_BLK_DEV + map_ref[2, t]
            key = jnp.where(t < count, key, slots)
            product = jnp.dot(src[:, pl.ds(begin, blk)], w[t], preferred_element_type=jnp.float32)
            acc = accs[j % len(accs)]
            acc[key] += product

    for slot in range(slots):
        total = accs[0][slot]
        for acc in accs[1:]:
            total = total + acc[slot]
        out_ref[slot] = total


def local_sums(source, weights, tile_map, tile_count):
    feat = source.shape[0]
    tiles, blk, _ = weights.shape
    devices = lax.axis_size("dev")
    chunk = CHUNK
    while tiles % chunk:
        chunk //= 2
    slots = (2 * REACH + 2) * ACU_BLK_DEV
    return pl.pallas_call(
        functools.partial(sums_kernel, devices, chunk),
        out_shape=jax.ShapeDtypeStruct((slots, feat, blk), jnp.float32),
        in_specs=[
            pl.BlockSpec(memory_space=pltpu.SMEM),
            pl.BlockSpec(memory_space=pltpu.SMEM),
            pl.BlockSpec(memory_space=pl.ANY),
            pl.BlockSpec(memory_space=pl.ANY),
        ],
        out_specs=pl.BlockSpec(memory_space=pltpu.VMEM),
        scratch_shapes=[
            pltpu.VMEM(source.shape, source.dtype),
            pltpu.VMEM(weights.shape, weights.dtype),
            pltpu.SMEM((devices,), jnp.int32),
            pltpu.SemaphoreType.DMA,
            pltpu.SemaphoreType.DMA((tiles // chunk,)),
        ]
        + [pltpu.VMEM((slots + 1, feat, blk), jnp.float32) for _ in range(COPIES)],
        name="local_sums",
    )(tile_map, tile_count, source, weights)


def on_device(source, weights, tile_map, tile_count):
    feat = source.shape[0]
    blk = weights.shape[1]
    acu = ACU_BLK_DEV
    devices = lax.axis_size("dev")
    far_slot = 2 * REACH + 1
    outgoing = local_sums(source, weights, tile_map, tile_count)
    outgoing = outgoing.reshape(2 * REACH + 2, acu, feat, blk)
    total = outgoing[REACH]
    for index in range(2 * REACH + 1):
        if index != REACH:
            total = total + passed_along(outgoing[index], "dev", index - REACH)
    total = total + passed_along(outgoing[far_slot], "dev", devices // 2)
    return jnp.transpose(total, (1, 0, 2)).reshape(feat, acu * blk)


def solution(mesh):
    return jax.shard_map(
        on_device,
        mesh=mesh,
        in_specs=(P(None, "dev"), P("dev", None, None), P(None, "dev"), P("dev")),
        out_specs=P(None, "dev"),
        check_vma=False,
    )
```

time: 107 us -> 32.7 us (0.31); the launches traced: 105 us -> 33 us
  other arithmetic: 63.7 us -> 1.37 us
  matrix products: 16.4 us -> 0 us
  Pallas kernels: 0 us -> 11.5 us
  local copies, waits for them, and re-layouts: 5.74 us -> 0.9 us
  starting transfers between devices: 14.1 us -> 12.9 us
    scatter-add x1 -> x0, other arithmetic: 62.2 us -> none  [on_device(): jax.ops.segment_sum(products, segment_key, num_segments=(2 * REACH + 2) *...]
    dot_general x1 -> x0, matrix products: 16.4 us -> none  [on_device(): jnp.einsum('ftc,tcn->tfn', picked, weights, preferred_element_type=jnp.fl...]
    pallas_call x0 -> x1, Pallas kernels: none -> 11.5 us  [local_sums(): pl.pallas_call(functools.partial(sums_kernel, devices, chunk), out_shape=...]
    gather x1 -> x0, local copies, waits for them, and re-layouts: 4.78 us -> none  [on_device(): picked = jnp.take(blocks, tile_map[0], axis=1)]
    ppermute x9, starting transfers between devices: 14.1 us -> 12.9 us  [passed_along(): return lax.ppermute(value, axis, pairs)]
where the time goes in v1:
time: 32.7 us; the launch traced here: 33 us
  starting transfers between devices  12.9 us (39%)
  Pallas kernels  11.5 us (35%)
  waiting for transfers between devices  5.63 us (17%)
  other arithmetic  1.37 us (4%)
  local copies, waits for them, and re-layouts  0.9 us (3%)
  between operations  0.68 us (2%)
    ppermute x9, starting transfers between devices, passed_along(): return lax.ppermute(value, axis, pairs)  12.9 us
    pallas_call x1, Pallas kernels, local_sums(): pl.pallas_call(functools.partial(sums_kernel, devices, chunk), out_shape=...  11.5 us
    ppermute x9, waiting for transfers between devices, passed_along(): return lax.ppermute(value, axis, pairs)  5.63 us
    another operation x1, other arithmetic, on_device(): return jnp.transpose(total, (1, 0, 2)).reshape(feat, acu * blk)  1.37 us
    slice x1, local copies, waits for them, and re-layouts, on_device(): total = total + passed_along(outgoing[index], 'dev', index - REACH)  0.9 us
  transfers between devices with their start and end apart: 9, of which 4 were waited for; matrix products, arithmetic and copies ran while one was open for 0% of the time, Pallas kernels for 0%

profile of v1, /device:TPU:0, one launch (start us, length us, event | category | flops | bytes accessed | tf_op | source)
XLA Modules:
  0.0 33.0 jit_solution(17106372677849089638)
XLA Ops:
  0.7 11.5 %local_sums.1 = f32[10,48,128]{2,1,0:T(8,128)} custom-call(s32[3,640]{1,0:T(4,128)} %map_ref.1, s32[1]{0:T(128)S(6)} %copy.5.count_ref, bf16[48,8192]{1,0:T(8,128)(2,1)} %src_hbm.1, bf16[640,128,128]{2,1,0:T(8,128)(2,1)} %w_hbm.1), custom_call_target="tpu_custom_call" | custom-call | tf_op jit(solution)/shard_map/local_sums/pallas_call | solution.py:78
  12.2 0.9 %fusion.9 = (f32[1,48,128]{2,1,0:T(8,128)S(1)}, f32[1,48,128]{2,1,0:T(8,128)S(1)}, f32[1,48,128]{2,1,0:T(8,128)S(1)}, f32[1,48,128]{2,1,0:T(8,128)S(1)}, f32[1,4...) fusion(f32[10,48,128]{2,1,0:T(8,128)} %local_sums.1), kind=kLoop, calls=%fused_computation.10 | loop fusion | bytes 442368 | tf_op jit(solution)/shard_map/slice | solution.py:111
  13.1 6.5 %collective-permute-start = (f32[1,48,128]{2,1,0:T(8,128)S(1)}, f32[1,48,128]{2,1,0:T(8,128)S(1)}, u32[]{:S(2)}, u32[]{:S(2)}) collective-permute-start(f32[1,48,128]{2,1,0:T(8,128)S(1)} %get-tuple-element.5), channel_id=1, source_target_pairs={{0,28},{1,29},{2,30},{3,31},{4,0},{5,1},{6,2},{7,3},{8,4},{9,5},{1... | collective-permute-start | bytes 73736 | tf_op jit(solution)/shard_map/ppermute | solution.py:19
  19.6 0.0 collective-permute-start.8
  19.6 0.0 collective-permute-start.7
  19.6 0.2 collective-permute-start.6
  19.9 0.9 %collective-permute-start.5 = (f32[1,48,128]{2,1,0:T(8,128)S(1)}, f32[1,48,128]{2,1,0:T(8,128)S(1)}, u32[]{:S(2)}, u32[]{:S(2)}) collective-permute-start(f32[1,48,128]{2,1,0:T(8,128)S(1)} %get-tuple-element.9), channel_id=1, source_target_pairs={{0,2},{1,3},{2,4},{3,5},{4,6},{5,7},{6,8},{7,9},{8,10},{9,11},{10,... | collective-permute-start | bytes 73736 | tf_op jit(solution)/shard_map/ppermute | solution.py:19
  20.7 0.4 %collective-permute-done = f32[1,48,128]{2,1,0:T(8,128)S(1)} collective-permute-done((f32[1,48,128]{2,1,0:T(8,128)S(1)}, f32[1,48,128]{2,1,0:T(8,128)S(1)}, u32[]{:S(2)}, u32[]{:S(2)}) %collective-permute-start) | collective-permute-done | bytes 24608 | tf_op jit(solution)/shard_map/ppermute | solution.py:19
  21.1 1.0 %collective-permute-start.4 = (f32[1,48,128]{2,1,0:T(8,128)S(1)}, f32[1,48,128]{2,1,0:T(8,128)S(1)}, u32[]{:S(2)}, u32[]{:S(2)}) collective-permute-start(f32[1,48,128]{2,1,0:T(8,128)S(1)} %get-tuple-element.10), channel_id=1, source_target_pairs={{0,1},{1,2},{2,3},{3,4},{4,5},{5,6},{6,7},{7,8},{8,9},{9,10},{10,1... | collective-permute-start | bytes 73736 | tf_op jit(solution)/shard_map/ppermute | solution.py:19
  22.2 2.2 %collective-permute-done.8 = f32[1,48,128]{2,1,0:T(8,128)S(1)} collective-permute-done((f32[1,48,128]{2,1,0:T(8,128)S(1)}, f32[1,48,128]{2,1,0:T(8,128)S(1)}, u32[]{:S(2)}, u32[]{:S(2)}) %collective-permute-start.8) | collective-permute-done | bytes 24608 | tf_op jit(solution)/shard_map/ppermute | solution.py:19
  24.3 2.1 %collective-permute-start.3 = (f32[1,48,128]{2,1,0:T(8,128)S(1)}, f32[1,48,128]{2,1,0:T(8,128)S(1)}, u32[]{:S(2)}, u32[]{:S(2)}) collective-permute-start(f32[1,48,128]{2,1,0:T(8,128)S(1)} %get-tuple-element.11), channel_id=1, source_target_pairs={{0,31},{1,0},{2,1},{3,2},{4,3},{5,4},{6,5},{7,6},{8,7},{9,8},{10,9... | collective-permute-start | bytes 73736 | tf_op jit(solution)/shard_map/ppermute | solution.py:19
  26.5 0.0 collective-permute-done.7
  26.5 1.9 %collective-permute-start.2 = (f32[1,48,128]{2,1,0:T(8,128)S(1)}, f32[1,48,128]{2,1,0:T(8,128)S(1)}, u32[]{:S(2)}, u32[]{:S(2)}) collective-permute-start(f32[1,48,128]{2,1,0:T(8,128)S(1)} %get-tuple-element.12), channel_id=1, source_target_pairs={{0,30},{1,31},{2,0},{3,1},{4,2},{5,3},{6,4},{7,5},{8,6},{9,7},{10,... | collective-permute-start | bytes 73736 | tf_op jit(solution)/shard_map/ppermute | solution.py:19
  28.4 0.0 collective-permute-done.6
  28.4 0.2 collective-permute-start.1
  28.6 0.0 collective-permute-done.5
  28.6 0.0 collective-permute-done.4
  28.6 0.0 collective-permute-done.3
  28.6 1.7 %collective-permute-done.2 = f32[1,48,128]{2,1,0:T(8,128)S(1)} collective-permute-done((f32[1,48,128]{2,1,0:T(8,128)S(1)}, f32[1,48,128]{2,1,0:T(8,128)S(1)}, u32[]{:S(2)}, u32[]{:S(2)}) %collective-permute-start.2) | collective-permute-done | bytes 24608 | tf_op jit(solution)/shard_map/ppermute | solution.py:19
  30.3 1.3 %collective-permute-done.1 = f32[1,48,128]{2,1,0:T(8,128)S(1)} collective-permute-done((f32[1,48,128]{2,1,0:T(8,128)S(1)}, f32[1,48,128]{2,1,0:T(8,128)S(1)}, u32[]{:S(2)}, u32[]{:S(2)}) %collective-permute-start.1) | collective-permute-done | bytes 24608 | tf_op jit(solution)/shard_map/ppermute | solution.py:19
  31.6 1.4 %fusion.8 = f32[48,128]{1,0:T(8,128)} fusion(f32[1,48,128]{2,1,0:T(8,128)S(1)} %collective-permute-done.8, f32[1,48,128]{2,1,0:T(8,128)S(1)} %collective-permute-done.7, f32[1,48,128]{2,1,0:T(8,128)S(1)} %collective-permute-done.6, f32[1,48,128]{2,1,0:T(8,128)S(1)} %collective-permute-done.5, f32[1,48,128]{2,1,0:T(8,128)S(1)} %collective-permute-done.4, ...), kind=kLoop, calls=%fused_computation.9 | loop fusion | flops 55296 | bytes 270336 | tf_op jit(solution)/shard_map/reshape;transpose | solution.py:113
Async XLA Ops:
  13.1 8.0 %collective-permute-start = (f32[1,48,128]{2,1,0:T(8,128)S(1)}, f32[1,48,128]{2,1,0:T(8,128)S(1)}, u32[]{:S(2)}, u32[]{:S(2)}) collective-permute-start(f32[1,48,128]{2,1,0:T(8,128)S(1)} %get-tuple-element.5), channel_id=1, source_target_pairs={{0,28},{1,29},{2,30},{3,31},{4,0},{5,1},{6,2},{7,3},{8,4},{9,5},{1... | collective-permute-start | bytes 73736 | tf_op jit(solution)/shard_map/ppermute | solution.py:19
  19.6 4.7 %collective-permute-start.8 = (f32[1,48,128]{2,1,0:T(8,128)S(1)}, f32[1,48,128]{2,1,0:T(8,128)S(1)}, u32[]{:S(2)}, u32[]{:S(2)}) collective-permute-start(f32[1,48,128]{2,1,0:T(8,128)S(1)} %get-tuple-element.6), channel_id=1, source_target_pairs={{0,16},{1,17},{2,18},{3,19},{4,20},{5,21},{6,22},{7,23},{8,24},{9,... | collective-permute-start | bytes 73736 | tf_op jit(solution)/shard_map/ppermute | solution.py:19
  19.6 6.9 %collective-permute-start.7 = (f32[1,48,128]{2,1,0:T(8,128)S(1)}, f32[1,48,128]{2,1,0:T(8,128)S(1)}, u32[]{:S(2)}, u32[]{:S(2)}) collective-permute-start(f32[1,48,128]{2,1,0:T(8,128)S(1)} %get-tuple-element.7), channel_id=1, source_target_pairs={{0,4},{1,5},{2,6},{3,7},{4,8},{5,9},{6,10},{7,11},{8,12},{9,13},{1... | collective-permute-start | bytes 73736 | tf_op jit(solution)/shard_map/ppermute | solution.py:19
  19.6 8.8 %collective-permute-start.6 = (f32[1,48,128]{2,1,0:T(8,128)S(1)}, f32[1,48,128]{2,1,0:T(8,128)S(1)}, u32[]{:S(2)}, u32[]{:S(2)}) collective-permute-start(f32[1,48,128]{2,1,0:T(8,128)S(1)} %get-tuple-element.8), channel_id=1, source_target_pairs={{0,3},{1,4},{2,5},{3,6},{4,7},{5,8},{6,9},{7,10},{8,11},{9,12},{10... | collective-permute-start | bytes 73736 | tf_op jit(solution)/shard_map/ppermute | solution.py:19
  19.9 8.7 %collective-permute-start.5 = (f32[1,48,128]{2,1,0:T(8,128)S(1)}, f32[1,48,128]{2,1,0:T(8,128)S(1)}, u32[]{:S(2)}, u32[]{:S(2)}) collective-permute-start(f32[1,48,128]{2,1,0:T(8,128)S(1)} %get-tuple-element.9), channel_id=1, source_target_pairs={{0,2},{1,3},{2,4},{3,5},{4,6},{5,7},{6,8},{7,9},{8,10},{9,11},{10,... | collective-permute-start | bytes 73736 | tf_op jit(solution)/shard_map/ppermute | solution.py:19
  21.1 7.4 %collective-permute-start.4 = (f32[1,48,128]{2,1,0:T(8,128)S(1)}, f32[1,48,128]{2,1,0:T(8,128)S(1)}, u32[]{:S(2)}, u32[]{:S(2)}) collective-permute-start(f32[1,48,128]{2,1,0:T(8,128)S(1)} %get-tuple-element.10), channel_id=1, source_target_pairs={{0,1},{1,2},{2,3},{3,4},{4,5},{5,6},{6,7},{7,8},{8,9},{9,10},{10,1... | collective-permute-start | bytes 73736 | tf_op jit(solution)/shard_map/ppermute | solution.py:19
  24.3 4.2 %collective-permute-start.3 = (f32[1,48,128]{2,1,0:T(8,128)S(1)}, f32[1,48,128]{2,1,0:T(8,128)S(1)}, u32[]{:S(2)}, u32[]{:S(2)}) collective-permute-start(f32[1,48,128]{2,1,0:T(8,128)S(1)} %get-tuple-element.11), channel_id=1, source_target_pairs={{0,31},{1,0},{2,1},{3,2},{4,3},{5,4},{6,5},{7,6},{8,7},{9,8},{10,9... | collective-permute-start | bytes 73736 | tf_op jit(solution)/shard_map/ppermute | solution.py:19
  26.5 3.8 %collective-permute-start.2 = (f32[1,48,128]{2,1,0:T(8,128)S(1)}, f32[1,48,128]{2,1,0:T(8,128)S(1)}, u32[]{:S(2)}, u32[]{:S(2)}) collective-permute-start(f32[1,48,128]{2,1,0:T(8,128)S(1)} %get-tuple-element.12), channel_id=1, source_target_pairs={{0,30},{1,31},{2,0},{3,1},{4,2},{5,3},{6,4},{7,5},{8,6},{9,7},{10,... | collective-permute-start | bytes 73736 | tf_op jit(solution)/shard_map/ppermute | solution.py:19
  28.4 3.3 %collective-permute-start.1 = (f32[1,48,128]{2,1,0:T(8,128)S(1)}, f32[1,48,128]{2,1,0:T(8,128)S(1)}, u32[]{:S(2)}, u32[]{:S(2)}) collective-permute-start(f32[1,48,128]{2,1,0:T(8,128)S(1)} %get-tuple-element.13), channel_id=1, source_target_pairs={{0,29},{1,30},{2,31},{3,0},{4,1},{5,2},{6,3},{7,4},{8,5},{9,6},{10... | collective-permute-start | bytes 73736 | tf_op jit(solution)/shard_map/ppermute | solution.py:19

commit v2 on v1

--- a/solution.py
+++ b/solution.py
@@ -13,10 +13,67 @@
 COPIES = 8
 
 
-def passed_along(value, axis, steps):
-    count = lax.axis_size(axis)
-    pairs = [(source, (source + steps) % count) for source in range(count)]
-    return lax.ppermute(value, axis, pairs)
+def near_and_far(devices):
+    pairs = []
+    if devices // 2 > REACH:
+        pairs.append((devices // 2, 2 * REACH + 1))
+    for step in range(REACH, 0, -1):
+        pairs += [(step, REACH + step), (-step, REACH - step)]
+    return pairs
+
+
+def exchange_kernel(devices, sums, out_ref, landed, send_sem, recv_sem):
+    acu = ACU_BLK_DEV
+    own = lax.axis_index("dev")
+    pairs = near_and_far(devices)
+    barrier = pltpu.get_barrier_semaphore()
+    for distance, _ in pairs:
+        pl.semaphore_signal(
+            barrier,
+            inc=1,
+            device_id=(lax.rem(own - distance + devices, devices),),
+            device_id_type=pl.DeviceIdType.MESH,
+        )
+    pl.semaphore_wait(barrier, len(pairs))
+    copies = []
+    for index, (distance, slot) in enumerate(pairs):
+        copies.append(
+            pltpu.make_async_remote_copy(
+                src_ref=sums.at[pl.ds(slot * acu, acu)],
+                dst_ref=landed.at[index],
+                send_sem=send_sem.at[index],
+                recv_sem=recv_sem.at[index],
+                device_id=(lax.rem(own + distance + devices, devices),),
+                device_id_type=pl.DeviceIdType.MESH,
+            )
+        )
+        copies[-1].start()
+    total = sums[pl.ds(REACH * acu, acu)]
+    for index in reversed(range(len(pairs))):
+        copies[index].wait_recv()
+        total = total + landed[index]
+    out_ref[...] = total
+    for copy in copies:
+        copy.wait_send()
+
+
+def exchanged(sums):
+    devices = lax.axis_size("dev")
+    _, feat, blk = sums.shape
+    flows = len(near_and_far(devices))
+    return pl.pallas_call(
+        functools.partial(exchange_kernel, devices),
+        out_shape=jax.ShapeDtypeStruct((ACU_BLK_DEV, feat, blk), jnp.float32),
+        in_specs=[pl.BlockSpec(memory_space=pltpu.VMEM)],
+        out_specs=pl.BlockSpec(memory_space=pltpu.VMEM),
+        scratch_shapes=[
+            pltpu.VMEM((flows, ACU_BLK_DEV, feat, blk), jnp.float32),
+            pltpu.SemaphoreType.DMA((flows,)),
+            pltpu.SemaphoreType.DMA((flows,)),
+        ],
+        compiler_params=pltpu.CompilerParams(collective_id=0, has_side_effects=True),
+        name="exchange",
+    )(sums)
 
 
 def sums_kernel(devices, chunk, map_ref, count_ref, src_hbm, w_hbm, out_ref, src, w, lut, src_sem, w_sem, *accs):
@@ -101,15 +158,7 @@
     feat = source.shape[0]
     blk = weights.shape[1]
     acu = ACU_BLK_DEV
-    devices = lax.axis_size("dev")
-    far_slot = 2 * REACH + 1
-    outgoing = local_sums(source, weights, tile_map, tile_count)
-    outgoing = outgoing.reshape(2 * REACH + 2, acu, feat, blk)
-    total = outgoing[REACH]
-    for index in range(2 * REACH + 1):
-        if index != REACH:
-            total = total + passed_along(outgoing[index], "dev", index - REACH)
-    total = total + passed_along(outgoing[far_slot], "dev", devices // 2)
+    total = exchanged(local_sums(source, weights, tile_map, tile_count))
     return jnp.transpose(total, (1, 0, 2)).reshape(feat, acu * blk)
 
 

time: 32.7 us -> 26 us (0.80); the launches traced: 33 us -> 25.5 us
  starting transfers between devices: 12.9 us -> 0 us
  Pallas kernels: 11.5 us -> 23.5 us
  waiting for transfers between devices: 5.63 us -> 0 us
  other arithmetic: 1.37 us -> 0 us
  local copies, waits for them, and re-layouts: 0.9 us -> 1.35 us
    ppermute x9 -> x0, starting transfers between devices: 12.9 us -> none  [passed_along(): return lax.ppermute(value, axis, pairs)]
    pallas_call x0 -> x1, Pallas kernels: none -> 11.9 us  [exchanged(): pl.pallas_call(functools.partial(exchange_kernel, devices), out_shape=jax...]
    ppermute x9 -> x0, waiting for transfers between devices: 5.63 us -> none  [passed_along(): return lax.ppermute(value, axis, pairs)]
    another operation x1 -> x0, other arithmetic: 1.37 us -> none  [on_device(): return jnp.transpose(total, (1, 0, 2)).reshape(feat, acu * blk)]
    unnamed x0 -> x1, local copies, waits for them, and re-layouts: none -> 1.35 us
    slice x1 -> x0, local copies, waits for them, and re-layouts: 0.9 us -> none  [on_device(): total = total + passed_along(outgoing[index], 'dev', index - REACH)]
  transfers between devices with their start and end apart: 9 -> 0, of which waited for: 4 -> 0; matrix products, arithmetic and copies ran while one was open for 0% -> 0% of each run, Pallas kernels for 0% -> 0%
where the time goes in v2:
time: 26 us; the launch traced here: 25.5 us
  Pallas kernels  23.5 us (90%)
  local copies, waits for them, and re-layouts  1.35 us (5%)
  between operations  0.67 us (3%)
    pallas_call x1, Pallas kernels, exchanged(): pl.pallas_call(functools.partial(exchange_kernel, devices), out_shape=jax...  11.9 us
    pallas_call x1, Pallas kernels, local_sums(): pl.pallas_call(functools.partial(sums_kernel, devices, chunk), out_shape=...  11.5 us
    unnamed x1, local copies, waits for them, and re-layouts  1.35 us

profile of v2, /device:TPU:0, one launch (start us, length us, event | category | flops | bytes accessed | tf_op | source)
XLA Modules:
  0.0 25.5 jit_solution(8922406275329685806)
XLA Ops:
  0.7 11.5 %local_sums.1.sums = f32[10,48,128]{2,1,0:T(8,128)} custom-call(s32[3,640]{1,0:T(4,128)} %map_ref.1, s32[1]{0:T(128)S(6)} %copy.6.count_ref, bf16[48,8192]{1,0:T(8,128)(2,1)} %src_hbm.1, bf16[640,128,128]{2,1,0:T(8,128)(2,1)} %w_hbm.1), custom_call_target="tpu_custom_call" | custom-call | tf_op jit(solution)/shard_map/local_sums/pallas_call | solution.py:135
  12.2 11.9 %exchange.1 = f32[1,48,128]{2,1,0:T(8,128)} custom-call(f32[10,48,128]{2,1,0:T(8,128)} %local_sums.1.sums), custom_call_target="tpu_custom_call" | custom-call | tf_op jit(solution)/shard_map/exchange/pallas_call | solution.py:64
  24.1 1.3 %copy.7 = f32[48,128]{1,0:T(8,128)} copy(f32[48,128]{1,0:T(8,128)} %bitcast.1) | data formatting | bytes 49152
